TPU v7x, 32 devices: a whole 2x2x4 slice. The times are simulated.
32 devices in a mesh: fsdp: 8 (over z, y), tp: 4 (over x, core).
Axes of the slice: x: 2, y: 2, z: 4, core: 2. Of those that a mesh axis runs over, the one named last changes fastest.
Arguments:
- block_in: bfloat16 [8192, 2048], P(('fsdp', 'tp')), may hold values from -6 to 6
- segment_ids: int32 [8192], P('fsdp'), may hold values from 0 to 31, never falling along the last dimension, each value on 1 to 512 neighbouring positions
- w_query: bfloat16 [2048, 2048], P('fsdp', 'tp'), may hold values from -0.125 to 0.125
- w_key: bfloat16 [2048, 2048], P('fsdp', 'tp'), may hold values from -0.125 to 0.125
- w_value: bfloat16 [2048, 2048], P('fsdp', 'tp'), may hold values from -0.125 to 0.125
- w_out: bfloat16 [2048, 2048], P('fsdp', 'tp'), may hold values from -0.125 to 0.125
- w_gate: bfloat16 [2048, 8192], P('fsdp', 'tp'), may hold values from -0.125 to 0.125
- w_up: bfloat16 [2048, 8192], P('fsdp', 'tp'), may hold values from -0.125 to 0.125
- w_down: bfloat16 [2048, 8192], P('fsdp', 'tp'), may hold values from -0.0625 to 0.0625
- gains: bfloat16 [4, 2048], replicated, may hold values from 0.25 to 1.75
- out_cotangent: bfloat16 [8192, 2048], P(('fsdp', 'tp')), may hold values from -18 to 18
Outputs:
- block_out: bfloat16 [8192, 2048], P(('fsdp', 'tp'))
- input_grad: bfloat16 [8192, 2048], P(('fsdp', 'tp'))
- query_grad: float32 [2048, 2048], P('fsdp', 'tp')
- key_grad: float32 [2048, 2048], P('fsdp', 'tp')
- value_grad: float32 [2048, 2048], P('fsdp', 'tp')
- output_grad: float32 [2048, 2048], P('fsdp', 'tp')
- gate_grad: float32 [2048, 8192], P('fsdp', 'tp')
- up_grad: float32 [2048, 8192], P('fsdp', 'tp')
- down_grad: float32 [2048, 8192], P('fsdp', 'tp')
- gains_grad: float32 [4, 2048], replicated
Inputs may be any that keep to these rules, and one draw needn't show every extreme that they name: `segment_ids`: segment ids never fall along the tokens; a segment covers 1 to 512 consecutive tokens.
All inputs are finite; a program needn't handle non-finite values.
Results may differ from a plain program's by a relative error of at most 0.02.
Values may be sent and summed in bfloat16 or wider, within the bound.
A program may use at most 192 MiB of HBM per device.

v0:
```python
import jax
import jax.numpy as jnp
from jax import lax
from jax.sharding import PartitionSpec as P

HD = 128
LEN = 1024
EPSILON = 1e-06
THETA = 500000.0
NEG_LARGE = -1e30


def dot_plain(left, right):
    return jnp.dot(left, right, preferred_element_type=jnp.float32)


def dot_rows(left, right):
    return lax.dot_general(
        left, right, (((1,), (1,)), ((), ())), preferred_element_type=jnp.float32
    )


def dot_cols(left, right):
    return lax.dot_general(
        left, right, (((0,), (0,)), ((), ())), preferred_element_type=jnp.float32
    )


def rotate_half(values):
    front_half = values[..., : HD // 2]
    back_half = values[..., HD // 2 :]
    return jnp.concatenate([-back_half, front_half], axis=-1)


def rotate_back(values):
    front_half = values[..., : HD // 2]
    back_half = values[..., HD // 2 :]
    return jnp.concatenate([back_half, -front_half], axis=-1)


def rotary(values, cosine, sine):
    return values * cosine + rotate_half(values) * sine


def unrotary(values, cosine, sine):
    return values * cosine + rotate_back(values * sine)


def rope_tables(row_count):
    positions = (jnp.arange(row_count, dtype=jnp.int32) % LEN).astype(jnp.float32)
    freq_index = jnp.arange(HD // 2, dtype=jnp.float32)
    frequency = THETA ** (-2.0 * freq_index / HD)
    angles = positions[:, None] * frequency[None, :]
    angles = jnp.concatenate([angles, angles], axis=1)[:, None, :]
    return (jnp.cos(angles), jnp.sin(angles))


def norm_back(unit_rows, scales, grad_unit):
    return scales * (
        grad_unit - unit_rows * jnp.mean(grad_unit * unit_rows, axis=-1, keepdims=True)
    )


def local(
    block_in,
    segment_ids,
    w_query,
    w_key,
    w_value,
    w_out,
    w_gate,
    w_up,
    w_down,
    gains,
    out_cotangent,
):
    tp_index = lax.axis_index("tp")
    model_width = block_in.shape[1]
    heads_width = w_query.shape[1]
    local_heads = heads_width // HD
    group_rows = segment_ids.shape[0]
    seq_count = group_rows // LEN
    block_rows = min(512, LEN)
    block_count = LEN // block_rows
    scale_factor = HD ** (-0.5)
    gain_values = gains.astype(jnp.float32)
    head_gains = lax.dynamic_slice_in_dim(gain_values, tp_index * heads_width, heads_width, 1)
    cosine, sine = rope_tables(group_rows)
    seq_ids = segment_ids.reshape(seq_count, LEN)
    key_positions = jnp.arange(LEN, dtype=jnp.int32)
    gathered_in = lax.all_gather(block_in, "tp", axis=0, tiled=True)
    weights_fwd = (
        lax.all_gather(w_query, "fsdp", axis=0, tiled=True),
        lax.all_gather(w_key, "fsdp", axis=0, tiled=True),
        lax.all_gather(w_value, "fsdp", axis=0, tiled=True),
        lax.all_gather(w_out, "fsdp", axis=0, tiled=True),
        lax.all_gather(w_gate, "fsdp", axis=0, tiled=True),
        lax.all_gather(w_up, "fsdp", axis=0, tiled=True),
        lax.all_gather(w_down, "fsdp", axis=0, tiled=True),
    )
    query_full, key_full, value_full, out_full, gate_full, up_full, down_full = weights_fwd
    query_raw = dot_plain(gathered_in, query_full)
    key_raw = dot_plain(gathered_in, key_full)
    value_low = dot_plain(gathered_in, value_full).astype(jnp.bfloat16)
    square_sums = lax.psum(
        (jnp.sum(query_raw * query_raw, axis=1), jnp.sum(key_raw * key_raw, axis=1)), "tp"
    )
    query_scale = lax.rsqrt(square_sums[0] / model_width + EPSILON)[:, None]
    key_scale = lax.rsqrt(square_sums[1] / model_width + EPSILON)[:, None]
    query_unit = query_raw * query_scale
    key_unit = key_raw * key_scale
    query_rot = rotary(
        (query_unit * head_gains[0]).reshape(group_rows, local_heads, HD), cosine, sine
    )
    key_rot = rotary((key_unit * head_gains[1]).reshape(group_rows, local_heads, HD), cosine, sine)
    query_seq = query_rot.astype(jnp.bfloat16).reshape(seq_count, LEN, local_heads, HD)
    key_seq = key_rot.astype(jnp.bfloat16).reshape(seq_count, LEN, local_heads, HD)
    value_seq = value_low.reshape(seq_count, LEN, local_heads, HD)

    def block_scores(seq_index, first_row):
        query_block = lax.dynamic_slice_in_dim(query_seq[seq_index], first_row, block_rows, 0)
        ids_row = seq_ids[seq_index]
        query_ids = lax.dynamic_slice_in_dim(ids_row, first_row, block_rows, 0)
        query_positions = first_row + jnp.arange(block_rows, dtype=jnp.int32)
        visible = (query_ids[:, None] == ids_row[None, :]) & (
            key_positions[None, :] <= query_positions[:, None]
        )
        scores = (
            jnp.einsum(
                "qhd,khd->hqk", query_block, key_seq[seq_index], preferred_element_type=jnp.float32
            )
            * scale_factor
        )
        return (jnp.where(visible[None, :, :], scores, NEG_LARGE), query_block)

    def attend_block(flat_index):
        seq_index = flat_index // block_count
        first_row = flat_index % block_count * block_rows
        scores, query_block = block_scores(seq_index, first_row)
        row_max = jnp.max(scores, axis=-1, keepdims=True)
        exponent = jnp.exp(scores - row_max)
        row_total = jnp.sum(exponent, axis=-1, keepdims=True)
        probs_low = (exponent / row_total).astype(jnp.bfloat16)
        context = jnp.einsum(
            "hqk,khd->qhd", probs_low, value_seq[seq_index], preferred_element_type=jnp.float32
        )
        return (context.astype(jnp.bfloat16), (row_max + jnp.log(row_total))[..., 0])

    contexts, log_totals = lax.map(
        attend_block, jnp.arange(seq_count * block_count, dtype=jnp.int32)
    )
    context_low = contexts.reshape(group_rows, heads_width)
    log_totals = log_totals.reshape(seq_count, block_count, local_heads, block_rows)
    attn_terms = dot_rows(context_low, out_full)
    attn_sum = lax.psum_scatter(attn_terms, "tp", scatter_dimension=0, tiled=True)
    attn_scale = lax.rsqrt(jnp.mean(attn_sum * attn_sum, axis=1, keepdims=True) + EPSILON)
    attn_unit = attn_sum * attn_scale
    hidden_mid = block_in.astype(jnp.float32) + attn_unit * gain_values[2]
    hidden_group = lax.all_gather(hidden_mid.astype(jnp.bfloat16), "tp", axis=0, tiled=True)
    gate_raw = dot_plain(hidden_group, gate_full)
    up_raw = dot_plain(hidden_group, up_full)
    sigmoid_gate = jax.nn.sigmoid(gate_raw)
    silu_gate = gate_raw * sigmoid_gate
    inner_low = (silu_gate * up_raw).astype(jnp.bfloat16)
    mlp_terms = dot_rows(inner_low, down_full)
    mlp_sum = lax.psum_scatter(mlp_terms, "tp", scatter_dimension=0, tiled=True)
    mlp_scale = lax.rsqrt(jnp.mean(mlp_sum * mlp_sum, axis=1, keepdims=True) + EPSILON)
    mlp_unit = mlp_sum * mlp_scale
    block_out = (hidden_mid + mlp_unit * gain_values[3]).astype(jnp.bfloat16)
    weights_bwd = (
        lax.all_gather(w_query, "fsdp", axis=0, tiled=True),
        lax.all_gather(w_key, "fsdp", axis=0, tiled=True),
        lax.all_gather(w_value, "fsdp", axis=0, tiled=True),
        lax.all_gather(w_out, "fsdp", axis=0, tiled=True),
        lax.all_gather(w_gate, "fsdp", axis=0, tiled=True),
        lax.all_gather(w_up, "fsdp", axis=0, tiled=True),
        lax.all_gather(w_down, "fsdp", axis=0, tiled=True),
    )
    query_back_w, key_back_w, value_back_w, out_back_w, gate_back_w, up_back_w, down_back_w = (
        weights_bwd
    )
    grad_final = out_cotangent.astype(jnp.float32)
    mlp_gain_term = jnp.sum(grad_final * mlp_unit, axis=0)
    mixed_back = norm_back(mlp_unit, mlp_scale, grad_final * gain_values[3]).astype(jnp.bfloat16)
    mixed_group = lax.all_gather(mixed_back, "tp", axis=0, tiled=True)
    inner_back = dot_plain(mixed_group, down_back_w)
    down_grad = dot_cols(mixed_group, inner_low)
    gate_back = (
        inner_back * up_raw * sigmoid_gate * (1.0 + gate_raw * (1.0 - sigmoid_gate))
    ).astype(jnp.bfloat16)
    up_back = (inner_back * silu_gate).astype(jnp.bfloat16)
    gate_grad = dot_cols(hidden_group, gate_back)
    up_grad = dot_cols(hidden_group, up_back)
    hidden_terms = dot_rows(gate_back, gate_back_w) + dot_rows(up_back, up_back_w)
    hidden_back = grad_final + lax.psum_scatter(hidden_terms, "tp", scatter_dimension=0, tiled=True)
    attn_gain_term = jnp.sum(hidden_back * attn_unit, axis=0)
    attention_back = norm_back(attn_unit, attn_scale, hidden_back * gain_values[2]).astype(
        jnp.bfloat16
    )
    attention_group = lax.all_gather(attention_back, "tp", axis=0, tiled=True)
    context_back = dot_plain(attention_group, out_back_w).astype(jnp.bfloat16)
    output_grad = dot_cols(attention_group, context_low)
    context_back_seq = context_back.reshape(seq_count, LEN, local_heads, HD)

    def sequence_back(seq_index):
        seq_values = value_seq[seq_index]
        seq_keys = key_seq[seq_index]

        def block_back(accum_pair, block_index):
            keys_back, values_back = accum_pair
            first_row = block_index * block_rows
            scores, query_block = block_scores(seq_index, first_row)
            prob_values = jnp.exp(scores - log_totals[seq_index, block_index][..., None])
            probs_low = prob_values.astype(jnp.bfloat16)
            grad_block = lax.dynamic_slice_in_dim(
                context_back_seq[seq_index], first_row, block_rows, 0
            )
            probs_back = jnp.einsum(
                "qhd,khd->hqk", grad_block, seq_values, preferred_element_type=jnp.float32
            )
            row_delta = jnp.sum(prob_values * probs_back, axis=-1, keepdims=True)
            scores_back = (prob_values * (probs_back - row_delta)).astype(jnp.bfloat16)
            query_part = (
                jnp.einsum(
                    "hqk,khd->qhd", scores_back, seq_keys, preferred_element_type=jnp.float32
                )
                * scale_factor
            )
            keys_back = (
                keys_back
                + jnp.einsum(
                    "hqk,qhd->khd", scores_back, query_block, preferred_element_type=jnp.float32
                )
                * scale_factor
            )
            values_back = values_back + jnp.einsum(
                "hqk,qhd->khd", probs_low, grad_block, preferred_element_type=jnp.float32
            )
            return ((keys_back, values_back), query_part)

        zeros_seq = jnp.zeros((LEN, local_heads, HD), jnp.float32)
        (keys_back, values_back), query_parts = lax.scan(
            block_back, (zeros_seq, zeros_seq), jnp.arange(block_count, dtype=jnp.int32)
        )
        return (query_parts.reshape(LEN, local_heads, HD), keys_back, values_back)

    rot_query_back, rot_key_back, value_parts = lax.map(
        sequence_back, jnp.arange(seq_count, dtype=jnp.int32)
    )
    query_norm_back = unrotary(rot_query_back.reshape(group_rows, local_heads, HD), cosine, sine)
    query_norm_back = query_norm_back.reshape(group_rows, heads_width)
    key_norm_back = unrotary(rot_key_back.reshape(group_rows, local_heads, HD), cosine, sine)
    key_norm_back = key_norm_back.reshape(group_rows, heads_width)
    value_back = value_parts.reshape(group_rows, heads_width).astype(jnp.bfloat16)
    query_gain_term = jnp.sum(query_norm_back * query_unit, axis=0)
    key_gain_term = jnp.sum(key_norm_back * key_unit, axis=0)
    query_unit_back = query_norm_back * head_gains[0]
    key_unit_back = key_norm_back * head_gains[1]
    dot_sums = lax.psum(
        (jnp.sum(query_unit_back * query_unit, axis=1), jnp.sum(key_unit_back * key_unit, axis=1)),
        "tp",
    )
    query_back = (
        query_scale * (query_unit_back - query_unit * (dot_sums[0] / model_width)[:, None])
    ).astype(jnp.bfloat16)
    key_back = (
        key_scale * (key_unit_back - key_unit * (dot_sums[1] / model_width)[:, None])
    ).astype(jnp.bfloat16)
    input_terms = (
        dot_rows(query_back, query_back_w)
        + dot_rows(key_back, key_back_w)
        + dot_rows(value_back, value_back_w)
    )
    input_back = lax.psum_scatter(
        input_terms.astype(jnp.bfloat16), "tp", scatter_dimension=0, tiled=True
    ).astype(jnp.float32)
    input_grad = (hidden_back + input_back).astype(jnp.bfloat16)
    query_grad = dot_cols(gathered_in, query_back)
    key_grad = dot_cols(gathered_in, key_back)
    value_grad = dot_cols(gathered_in, value_back)
    weight_sums = (
        lax.psum_scatter(
            query_grad.astype(jnp.bfloat16), "fsdp", scatter_dimension=0, tiled=True
        ).astype(jnp.float32),
        lax.psum_scatter(
            key_grad.astype(jnp.bfloat16), "fsdp", scatter_dimension=0, tiled=True
        ).astype(jnp.float32),
        lax.psum_scatter(
            value_grad.astype(jnp.bfloat16), "fsdp", scatter_dimension=0, tiled=True
        ).astype(jnp.float32),
        lax.psum_scatter(
            output_grad.astype(jnp.bfloat16), "fsdp", scatter_dimension=0, tiled=True
        ).astype(jnp.float32),
        lax.psum_scatter(
            gate_grad.astype(jnp.bfloat16), "fsdp", scatter_dimension=0, tiled=True
        ).astype(jnp.float32),
        lax.psum_scatter(
            up_grad.astype(jnp.bfloat16), "fsdp", scatter_dimension=0, tiled=True
        ).astype(jnp.float32),
        lax.psum_scatter(
            down_grad.astype(jnp.bfloat16), "fsdp", scatter_dimension=0, tiled=True
        ).astype(jnp.float32),
    )
    head_terms = jnp.stack([query_gain_term, key_gain_term])
    placed = lax.dynamic_update_slice(
        jnp.zeros((2, model_width), jnp.float32), head_terms, (jnp.int32(0), tp_index * heads_width)
    )
    gain_terms = jnp.concatenate([placed, jnp.stack([attn_gain_term, mlp_gain_term])], axis=0)
    gains_grad = lax.psum(gain_terms, ("fsdp", "tp"))
    return (
        block_out,
        input_grad,
        weight_sums[0],
        weight_sums[1],
        weight_sums[2],
        weight_sums[3],
        weight_sums[4],
        weight_sums[5],
        weight_sums[6],
        gains_grad,
    )


def solution(mesh):
    in_specs = (
        P(("fsdp", "tp"), None),
        P("fsdp"),
        P("fsdp", "tp"),
        P("fsdp", "tp"),
        P("fsdp", "tp"),
        P("fsdp", "tp"),
        P("fsdp", "tp"),
        P("fsdp", "tp"),
        P("fsdp", "tp"),
        P(),
        P(("fsdp", "tp"), None),
    )
    out_specs = (
        P(("fsdp", "tp"), None),
        P(("fsdp", "tp"), None),
        P("fsdp", "tp"),
        P("fsdp", "tp"),
        P("fsdp", "tp"),
        P("fsdp", "tp"),
        P("fsdp", "tp"),
        P("fsdp", "tp"),
        P("fsdp", "tp"),
        P(),
    )
    return jax.shard_map(local, mesh=mesh, in_specs=in_specs, out_specs=out_specs, check_vma=False)
```

profile of v0, /device:TPU:0, one launch (start us, length us, event | category | flops | bytes accessed | tf_op | source)
XLA Modules:
  0.0 1814.4 jit_solution(8109534931990387546)
XLA Ops:
  13.2 48.7 %all-gather.14.cloned.1.call-done = bf16[2048,512]{1,0:T(8,128)(2,1)} async-done(((bf16[256,512]{1,0:T(8,128)(2,1)}), bf16[2048,512]{1,0:T(8,128)(2,1)}) %all-gather.14.cloned.1.call-update) | async-done | bytes 2097168 | tf_op jit(solution)/shard_map/all_gather | solution.py:93
  62.0 34.6 %all-gather.12.cloned.1.call-done = bf16[1024,2048]{1,0:T(8,128)(2,1)} async-done(((bf16[256,2048]{1,0:T(8,128)(2,1)}), bf16[1024,2048]{1,0:T(8,128)(2,1)}) %all-gather.12.cloned.1.call-update) | async-done | bytes 4194320 | tf_op jit(solution)/shard_map/all_gather | solution.py:91
  103.1 44.7 %all-gather.16.cloned.1.call-done = bf16[2048,512]{1,0:T(8,128)(2,1)} async-done(((bf16[256,512]{1,0:T(8,128)(2,1)}), bf16[2048,512]{1,0:T(8,128)(2,1)}) %all-gather.16.cloned.1.call-update) | async-done | bytes 2097168 | tf_op jit(solution)/shard_map/all_gather | solution.py:94
  180.3 17.1 all-gather.18.cloned.1.call-done
  210.2 23.4 %while.42 = (s32[]{:T(128)}, bf16[2,512,4,128]{3,2,1,0:T(4,128)(2,1)}, f32[2,4,512]{2,1,0:T(4,128)S(1)}, s32[2]{0:T(128)S(1)}, s32[1,1024]{1,0:T(1,128)S(1)}, /*...) while((s32[]{:T(128)}, ...), condition=%wide.region_7.8_spmd.clone, body=%wide.region_4.7_spmd.clone.sunk | while | flops 1100741120 | bytes 35732304 | solution.py:149
  255.5 69.3 %reduce-scatter.12.cloned.1.call-done = f32[256,2048]{1,0:T(8,128)} async-done(((f32[1024,2048]{1,0:T(8,128)}), f32[256,2048]{1,0:T(8,128)}) %reduce-scatter.12.cloned.1.call-update) | async-done | bytes 2097168 | tf_op jit(solution)/shard_map/reduce_scatter | solution.py:155
  329.8 121.7 %all-gather.24.cloned.1.call-done = bf16[2048,2048]{1,0:T(8,128)(2,1)} async-done(((bf16[256,2048]{1,0:T(8,128)(2,1)}), bf16[2048,2048]{1,0:T(8,128)(2,1)}) %all-gather.24.cloned.1.call-update) | async-done | bytes 8388624 | tf_op jit(solution)/shard_map/all_gather | solution.py:97
  451.4 34.8 %all-gather.22.cloned.1.call-done = bf16[1024,2048]{1,0:T(8,128)(2,1)} async-done(((bf16[256,2048]{1,0:T(8,128)(2,1)}), bf16[1024,2048]{1,0:T(8,128)(2,1)}) %all-gather.22.cloned.1.call-update) | async-done | bytes 4194320 | tf_op jit(solution)/shard_map/all_gather | solution.py:159
  501.2 111.7 %all-gather.26.cloned.1.call-done = bf16[2048,2048]{1,0:T(8,128)(2,1)} async-done(((bf16[256,2048]{1,0:T(8,128)(2,1)}), bf16[2048,2048]{1,0:T(8,128)(2,1)}) %all-gather.26.cloned.1.call-update) | async-done | bytes 8388624 | tf_op jit(solution)/shard_map/all_gather | solution.py:98
  612.9 17.0 multiply_convert_fusion.3
  629.9 107.7 %all-gather.28.cloned.1.call-done = bf16[2048,2048]{1,0:T(8,128)(2,1)} async-done(((bf16[256,2048]{1,0:T(8,128)(2,1)}), bf16[2048,2048]{1,0:T(8,128)(2,1)}) %all-gather.28.cloned.1.call-update) | async-done | bytes 8388624 | tf_op jit(solution)/shard_map/all_gather | solution.py:99
  752.3 69.7 %reduce-scatter.14.cloned.1.call-done = f32[256,2048]{1,0:T(8,128)} async-done(((f32[1024,2048]{1,0:T(8,128)}), f32[256,2048]{1,0:T(8,128)}) %reduce-scatter.14.cloned.1.call-update) | async-done | bytes 2097168 | tf_op jit(solution)/shard_map/reduce_scatter | solution.py:166
  827.1 34.6 %all-gather.30.cloned.1.call-done = bf16[1024,2048]{1,0:T(8,128)(2,1)} async-done(((bf16[256,2048]{1,0:T(8,128)(2,1)}), bf16[1024,2048]{1,0:T(8,128)(2,1)}) %all-gather.30.cloned.1.call-update) | async-done | bytes 4194320 | tf_op jit(solution)/shard_map/all_gather | solution.py:185
  861.6 19.9 %multiply_convert_fusion.1 = (bf16[1024,2048]{1,0:T(8,128)(2,1)S(1)}, bf16[1024,2048]{1,0:T(8,128)(2,1)}) fusion(f32[1024,2048]{1,0:T(8,128)} %fusion.81, f32[1024,2048]{1,0:T(8,128)} %get-tuple-element.465, bf16[1024,2048]{1,0:T(8,128)(2,1)} %all-gather.30.cloned.1.call-done, bf16[2048,2048]{1,0:T(8,128)(2,1)} %all-gather.28.cloned.1.call-done), kind=kOutput, calls=%fused_computation.61 | convolution fusion | flops 8617197568 | bytes 37748736 | tf_op jit(solution)/shard_map/dot_general | solution.py:14
  909.5 71.3 %reduce-scatter.16.cloned.1.call-done = f32[256,2048]{1,0:T(8,128)} async-done(((f32[1024,2048]{1,0:T(8,128)}), f32[256,2048]{1,0:T(8,128)}) %reduce-scatter.16.cloned.1.call-update) | async-done | bytes 2097168 | tf_op jit(solution)/shard_map/reduce_scatter | solution.py:195
  1044.5 68.7 %while.43 = (s32[]{:T(128)}, f32[1024,4,128]{0,2,1:T(8,128)S(1)}, f32[1024,4,128]{0,2,1:T(8,128)}, f32[2,512,4,128]{3,1,2,0:T(8,128)}, s32[2]{0:T(128)S(1)}, /*i...) while((s32[]{:T(128)}, f32[1024,4,128]{0,2,1:T(8,128)S(1)}, ...), condition=%wide.region_17.18_spmd.clone, body=%wide.region_15.17_spmd.clone.sunk | while | flops 2720266752 | bytes 163650544 | solution.py:242
  1192.0 130.0 %reduce-scatter.28.cloned.1.call-done = bf16[256,2048]{1,0:T(8,128)(2,1)} async-done(((bf16[2048,2048]{1,0:T(8,128)(2,1)}), bf16[256,2048]{1,0:T(8,128)(2,1)}) %reduce-scatter.28.cloned.1.call-update) | async-done | bytes 1048592 | tf_op jit(solution)/shard_map/reduce_scatter | solution.py:294
  1324.8 147.3 %reduce-scatter.30.cloned.1.call-done = bf16[256,2048]{1,0:T(8,128)(2,1)} async-done(((bf16[2048,2048]{1,0:T(8,128)(2,1)}), bf16[256,2048]{1,0:T(8,128)(2,1)}) %reduce-scatter.30.cloned.1.call-update) | async-done | bytes 1048592 | tf_op jit(solution)/shard_map/reduce_scatter | solution.py:297
  1475.0 40.9 %psum.39 = f32[4,2048]{1,0:T(4,128)} all-reduce(f32[4,2048]{1,0:T(4,128)S(1)} %pad_maximum_fusion.2), channel_id=1, replica_groups=mesh['fsdp'=8,'tp'=4] {'fsdp','tp'}, use_global_device_ids=true, to_apply=%region_34.35 | all-reduce | flops 8192 | bytes 65536 | tf_op jit(solution)/shard_map/psum | solution.py:309
  1515.9 28.3 %reduce-scatter.22.cloned.1.call-done = bf16[256,512]{0,1:T(8,128)(2,1)} async-done(((bf16[2048,512]{0,1:T(8,128)(2,1)}), bf16[256,512]{0,1:T(8,128)(2,1)}) %reduce-scatter.22.cloned.1.call-update) | async-done | bytes 262160 | tf_op jit(solution)/shard_map/reduce_scatter | solution.py:285
  1546.1 69.6 %reduce-scatter.20.cloned.1.call-done = bf16[256,512]{0,1:T(8,128)(2,1)} async-done(((bf16[2048,512]{0,1:T(8,128)(2,1)}), bf16[256,512]{0,1:T(8,128)(2,1)}) %reduce-scatter.20.cloned.1.call-update) | async-done | bytes 262160 | tf_op jit(solution)/shard_map/reduce_scatter | solution.py:282
  1617.6 69.0 %reduce-scatter.26.cloned.1.call-done = bf16[256,512]{1,0:T(8,128)(2,1)} async-done(((bf16[2048,512]{1,0:T(8,128)(2,1)}), bf16[256,512]{1,0:T(8,128)(2,1)}) %reduce-scatter.26.cloned.1.call-update) | async-done | bytes 262160 | tf_op jit(solution)/shard_map/reduce_scatter | solution.py:291
  1688.4 69.9 %reduce-scatter.24.cloned.1.call-done = bf16[256,512]{0,1:T(8,128)(2,1)} async-done(((bf16[2048,512]{0,1:T(8,128)(2,1)}), bf16[256,512]{0,1:T(8,128)(2,1)}) %reduce-scatter.24.cloned.1.call-update) | async-done | bytes 262160 | tf_op jit(solution)/shard_map/reduce_scatter | solution.py:288
  1760.1 44.3 %reduce-scatter.18.cloned.1.call-done = bf16[256,2048]{1,0:T(8,128)(2,1)} async-done(((bf16[1024,2048]{1,0:T(8,128)(2,1)}), bf16[256,2048]{1,0:T(8,128)(2,1)}) %reduce-scatter.18.cloned.1.call-update) | async-done | bytes 1048592 | tf_op jit(solution)/shard_map/reduce_scatter | solution.py:274
  (315 shorter events, 387.4 us)
Async XLA Ops:
  7.2 54.8 %all-gather.14.cloned.1.call-start = ((), (), s32[]{:S(2)}) async-start(), calls=%async_computation.12 | async-start | bytes 2359296 | tf_op jit(solution)/shard_map/all_gather | solution.py:93
  7.9 88.6 %all-gather.12.cloned.1.call-start = ((), (), s32[]{:S(2)}) async-start(), calls=%async_computation.11 | async-start | bytes 5242880 | tf_op jit(solution)/shard_map/all_gather | solution.py:91
  8.7 139.1 %all-gather.16.cloned.1.call-start = ((), (), s32[]{:S(2)}) async-start(), calls=%async_computation.13 | async-start | bytes 2359296 | tf_op jit(solution)/shard_map/all_gather | solution.py:94
  9.4 188.0 %all-gather.18.cloned.1.call-start = ((), (), s32[]{:S(2)}) async-start(), calls=%async_computation.14 | async-start | bytes 2359296 | tf_op jit(solution)/shard_map/all_gather | solution.py:95
  10.0 237.1 %all-gather.20.cloned.1.call-start = ((), (), s32[]{:S(2)}) async-start(), calls=%async_computation.15 | async-start | bytes 2359296 | tf_op jit(solution)/shard_map/all_gather | solution.py:96
  10.6 314.2 %reduce-scatter.12.cloned.1.call-start = ((), (), s32[]{:S(2)}) async-start(), calls=%async_computation.16 | async-start | bytes 10485760 | tf_op jit(solution)/shard_map/reduce_scatter | solution.py:155
  254.7 196.8 %all-gather.24.cloned.1.call-start = ((), (), s32[]{:S(2)}) async-start(), calls=%async_computation.18 | async-start | bytes 9437184 | tf_op jit(solution)/shard_map/all_gather | solution.py:97
  255.4 230.8 %all-gather.22.cloned.1.call-start = ((), (), s32[]{:S(2)}) async-start(), calls=%async_computation.17 | async-start | bytes 5242880 | tf_op jit(solution)/shard_map/all_gather | solution.py:159
  328.4 284.5 %all-gather.26.cloned.1.call-start = ((), (), s32[]{:S(2)}) async-start(), calls=%async_computation.19 | async-start | bytes 9437184 | tf_op jit(solution)/shard_map/all_gather | solution.py:98
  329.1 408.4 %all-gather.28.cloned.1.call-start = ((), (), s32[]{:S(2)}) async-start(), calls=%async_computation.20 | async-start | bytes 9437184 | tf_op jit(solution)/shard_map/all_gather | solution.py:99
  329.7 492.2 %reduce-scatter.14.cloned.1.call-start = ((), (), s32[]{:S(2)}) async-start(), calls=%async_computation.21 | async-start | bytes 10485760 | tf_op jit(solution)/shard_map/reduce_scatter | solution.py:166
  752.2 109.4 %all-gather.30.cloned.1.call-start = ((), (), s32[]{:S(2)}) async-start(), calls=%async_computation.22 | async-start | bytes 5242880 | tf_op jit(solution)/shard_map/all_gather | solution.py:185
  827.0 153.8 %reduce-scatter.16.cloned.1.call-start = ((), (), s32[]{:S(2)}) async-start(), calls=%async_computation.23 | async-start | bytes 10485760 | tf_op jit(solution)/shard_map/reduce_scatter | solution.py:195
  909.2 128.9 %all-gather.32.cloned.1.call-start = ((), (), s32[]{:S(2)}) async-start(), calls=%async_computation.24 | async-start | bytes 5242880 | tf_op jit(solution)/shard_map/all_gather | solution.py:200
  986.4 202.9 %reduce-scatter.32.cloned.1.call-start = ((), (), s32[]{:S(2)}) async-start(), calls=%async_computation.32 | async-start | bytes 9437184 | tf_op jit(solution)/shard_map/reduce_scatter | solution.py:300
  1000.5 321.5 %reduce-scatter.28.cloned.1.call-start = ((), (), s32[]{:S(2)}) async-start(), calls=%async_computation.30 | async-start | bytes 9437184 | tf_op jit(solution)/shard_map/reduce_scatter | solution.py:294
  1014.6 457.5 %reduce-scatter.30.cloned.1.call-start = ((), (), s32[]{:S(2)}) async-start(), calls=%async_computation.31 | async-start | bytes 9437184 | tf_op jit(solution)/shard_map/reduce_scatter | solution.py:297
  1029.2 515.0 %reduce-scatter.22.cloned.1.call-start = ((), (), s32[]{:S(2)}) async-start(), calls=%async_computation.27 | async-start | bytes 2359296 | tf_op jit(solution)/shard_map/reduce_scatter | solution.py:285
  1155.1 460.5 %reduce-scatter.20.cloned.1.call-start = ((), (), s32[]{:S(2)}) async-start(), calls=%async_computation.26 | async-start | bytes 2359296 | tf_op jit(solution)/shard_map/reduce_scatter | solution.py:282
  1162.1 524.5 %reduce-scatter.26.cloned.1.call-start = ((), (), s32[]{:S(2)}) async-start(), calls=%async_computation.29 | async-start | bytes 2359296 | tf_op jit(solution)/shard_map/reduce_scatter | solution.py:291
  1168.7 589.6 %reduce-scatter.24.cloned.1.call-start = ((), (), s32[]{:S(2)}) async-start(), calls=%async_computation.28 | async-start | bytes 2359296 | tf_op jit(solution)/shard_map/reduce_scatter | solution.py:288
  1176.4 628.0 %reduce-scatter.18.cloned.1.call-start = ((), (), s32[]{:S(2)}) async-start(), calls=%async_computation.25 | async-start | bytes 5242880 | tf_op jit(solution)/shard_map/reduce_scatter | solution.py:274
  1474.9 329.6 %copy-start.12 = (bf16[256,2048]{1,0:T(8,128)(2,1)S(1)}, bf16[256,2048]{1,0:T(8,128)(2,1)}, u32[]{:S(2)}) copy-start(bf16[256,2048]{1,0:T(8,128)(2,1)} %param.25) | copy-start | bytes 3145732
  1474.9 329.6 %copy-start.20 = (f32[256,2048]{1,0:T(8,128)S(1)}, f32[256,2048]{1,0:T(8,128)}, u32[]{:S(2)}) copy-start(f32[256,2048]{1,0:T(8,128)} %reduce-scatter.16.cloned.1.call-done) | copy-start | bytes 6291460
  (65 other events, 1430.1 us)
Sparse Core Ops, SparseCore 0:
  10.1 51.7 all-gather.13
  63.5 32.9 all-gather.11
  98.7 49.0 all-gather.15
  149.8 47.6 all-gather.17
  199.4 47.5 all-gather.19
  254.8 69.9 reduce-scatter.11
  326.9 124.4 all-gather.23
  453.6 32.6 all-gather.21
  488.4 124.4 all-gather.25
  614.9 122.6 all-gather.27
  752.3 69.5 reduce-scatter.13
  827.2 34.4 all-gather.29
  909.3 71.4 reduce-scatter.15
  986.5 34.4 all-gather.31
  1024.4 147.4 reduce-scatter.31
  1175.4 146.5 reduce-scatter.27
  1325.5 146.5 reduce-scatter.29
  1475.5 68.6 reduce-scatter.21
  1547.7 67.9 reduce-scatter.19
  1619.1 67.5 reduce-scatter.25
  1690.1 68.0 reduce-scatter.23
  1760.8 43.6 reduce-scatter.17
where the time goes:
time: 1820 us; the launch traced here: 1810 us
  waiting for transfers between devices  1340 us (74%)
  matrix products  261 us (14%)
  other arithmetic  78.8 us (4%)
  blocking collectives  53.6 us (3%)
  local copies, waits for them, and re-layouts  51.2 us (3%)
    reduce_scatter x1, waiting for transfers between devices, local(): lax.psum_scatter(up_grad.astype(jnp.bfloat16), 'fsdp', scatter_dimension=...  147 us
    reduce_scatter x1, waiting for transfers between devices, local(): lax.psum_scatter(gate_grad.astype(jnp.bfloat16), 'fsdp', scatter_dimensio...  130 us
    all_gather x1, waiting for transfers between devices, local(): lax.all_gather(w_gate, 'fsdp', axis=0, tiled=True)  122 us
    all_gather x1, waiting for transfers between devices, local(): lax.all_gather(w_up, 'fsdp', axis=0, tiled=True)  112 us
    all_gather x1, waiting for transfers between devices, local(): lax.all_gather(w_down, 'fsdp', axis=0, tiled=True)  108 us
    dot_general x7, matrix products, dot_plain(): return jnp.dot(left, right, preferred_element_type=jnp.float32)  75.3 us
    reduce_scatter x1, waiting for transfers between devices, local(): lax.psum_scatter(hidden_terms, 'tp', scatter_dimension=0, tiled=True)  71.3 us
    reduce_scatter x1, waiting for transfers between devices, local(): lax.psum_scatter(value_grad.astype(jnp.bfloat16), 'fsdp', scatter_dimensi...  69.9 us
  transfers between devices with their start and end apart: 22, of which 20 were waited for; matrix products, arithmetic and copies ran while one was open for 17% of the time, Pallas kernels for 0%

commit v1 on v0

--- a/solution.py
+++ b/solution.py
@@ -89,13 +89,43 @@
     seq_ids = segment_ids.reshape(seq_count, LEN)
     key_positions = jnp.arange(LEN, dtype=jnp.int32)
     gathered_in = lax.all_gather(block_in, "tp", axis=0, tiled=True)
+
+    def show_forms(z, lane_axis):
+        after = lax.axis_size(lane_axis)
+        local_next = lax.axis_index(lane_axis)
+        built, next_value, piece_next = (after, local_next, z.shape[0])
+        xs_all = []
+        for dev, ii in enumerate(z.shape):
+            xs_all.append(ii * built if dev == 0 else ii)
+        current_block = lax.dynamic_update_slice_in_dim(
+            jnp.zeros(xs_all, z.dtype), z, next_value * piece_next, axis=0
+        )
+        y = latest = z
+        for it in [*range(1, built // 2 + 1)]:
+            crops = []
+            for dev in tuple(range(built)):
+                crops.append((dev, (dev + 1) % built))
+            y = lax.ppermute(y, axis_name=lane_axis, perm=crops)
+            current_block = lax.dynamic_update_slice_in_dim(
+                current_block, y, (next_value - it) % built * piece_next, axis=0
+            )
+            if 2 * it < built:
+                cards = []
+                for dev in [*range(built)]:
+                    cards.append((dev, (dev - 1) % built))
+                latest = lax.ppermute(latest, axis_name=lane_axis, perm=cards)
+                current_block = lax.dynamic_update_slice_in_dim(
+                    current_block, latest, (next_value + it) % built * piece_next, axis=0
+                )
+        return current_block
+
     weights_fwd = (
         lax.all_gather(w_query, "fsdp", axis=0, tiled=True),
         lax.all_gather(w_key, "fsdp", axis=0, tiled=True),
         lax.all_gather(w_value, "fsdp", axis=0, tiled=True),
         lax.all_gather(w_out, "fsdp", axis=0, tiled=True),
         lax.all_gather(w_gate, "fsdp", axis=0, tiled=True),
-        lax.all_gather(w_up, "fsdp", axis=0, tiled=True),
+        show_forms(w_up, "fsdp"),
         lax.all_gather(w_down, "fsdp", axis=0, tiled=True),
     )
     query_full, key_full, value_full, out_full, gate_full, up_full, down_full = weights_fwd

time: 1820 us -> 1900 us (1.044)
  waiting for transfers between devices: 1340 us -> 1380 us
  starting transfers between devices: 1.75 us -> 31.8 us
  local copies, waits for them, and re-layouts: 51.2 us -> 72.2 us
    ppermute x0 -> x7, waiting for transfers between devices: none -> 191 us  [the longest x4 189 us: show_forms(): y = lax.ppermute(y, axis_name=lane_axis, perm=crops)]
    all_gather x1, waiting for transfers between devices: 122 us -> 0.01 us  [local(): lax.all_gather(w_gate, 'fsdp', axis=0, tiled=True)]
    ppermute x0 -> x7, starting transfers between devices: none -> 30 us  [the longest x3 21.1 us: show_forms(): latest = lax.ppermute(latest, axis_name=lane_axis, perm=cards)]
    all_gather x1, waiting for transfers between devices: 112 us -> 91.5 us  [local(): lax.all_gather(w_up, 'fsdp', axis=0, tiled=True)]
  transfers between devices with their start and end apart: 22 -> 29, of which waited for: 20 -> 24; matrix products, arithmetic and copies ran while one was open for 17% -> 18% of each run, Pallas kernels for 0% -> 0%
where the time goes in v1:
time: 1900 us
  waiting for transfers between devices  1380 us (73%)
  matrix products  258 us (14%)
  other arithmetic  78.7 us (4%)
  local copies, waits for them, and re-layouts  72.2 us (4%)
  blocking collectives  53.4 us (3%)
  starting transfers between devices  31.8 us (2%)
    ppermute x4, waiting for transfers between devices, show_forms(): y = lax.ppermute(y, axis_name=lane_axis, perm=crops)  189 us
    reduce_scatter x1, waiting for transfers between devices, local(): lax.psum_scatter(up_grad.astype(jnp.bfloat16), 'fsdp', scatter_dimension=...  147 us
    reduce_scatter x1, waiting for transfers between devices, local(): lax.psum_scatter(gate_grad.astype(jnp.bfloat16), 'fsdp', scatter_dimensio...  130 us
    all_gather x1, waiting for transfers between devices, local(): lax.all_gather(w_down, 'fsdp', axis=0, tiled=True)  95.2 us
    all_gather x1, waiting for transfers between devices, local(): lax.all_gather(w_up, 'fsdp', axis=0, tiled=True)  91.5 us
    dot_general x7, matrix products, dot_plain(): return jnp.dot(left, right, preferred_element_type=jnp.float32)  71.3 us
    reduce_scatter x1, waiting for transfers between devices, local(): lax.psum_scatter(value_grad.astype(jnp.bfloat16), 'fsdp', scatter_dimensi...  69.7 us
    reduce_scatter x1, waiting for transfers between devices, local(): mlp_sum = lax.psum_scatter(mlp_terms, 'tp', scatter_dimension=0, tiled=True)  69.7 us
  transfers between devices with their start and end apart: 29, of which 24 were waited for; matrix products, arithmetic and copies ran while one was open for 18% of the time, Pallas kernels for 0%

profile of v1, /device:TPU:0, one launch (start us, length us, event | category | flops | bytes accessed | tf_op | source)
XLA Modules:
  0.0 1896.3 jit_solution(4167739632740441464)
XLA Ops:
  13.2 48.7 %all-gather.14.cloned.1.call-done = bf16[2048,512]{1,0:T(8,128)(2,1)} async-done(((bf16[256,512]{1,0:T(8,128)(2,1)}), bf16[2048,512]{1,0:T(8,128)(2,1)}) %all-gather.14.cloned.1.call-update) | async-done | bytes 2097168 | tf_op jit(solution)/shard_map/all_gather | solution.py:123
  62.0 34.6 %all-gather.12.cloned.1.call-done = bf16[1024,2048]{1,0:T(8,128)(2,1)} async-done(((bf16[256,2048]{1,0:T(8,128)(2,1)}), bf16[1024,2048]{1,0:T(8,128)(2,1)}) %all-gather.12.cloned.1.call-update) | async-done | bytes 4194320 | tf_op jit(solution)/shard_map/all_gather | solution.py:91
  103.1 44.7 %all-gather.16.cloned.1.call-done = bf16[2048,512]{1,0:T(8,128)(2,1)} async-done(((bf16[256,512]{1,0:T(8,128)(2,1)}), bf16[2048,512]{1,0:T(8,128)(2,1)}) %all-gather.16.cloned.1.call-update) | async-done | bytes 2097168 | tf_op jit(solution)/shard_map/all_gather | solution.py:124
  210.1 23.9 %while.42 = (s32[]{:T(128)}, bf16[2,512,4,128]{3,2,1,0:T(4,128)(2,1)}, f32[2,4,512]{2,1,0:T(4,128)S(1)}, s32[2]{0:T(128)S(1)}, s32[1,1024]{1,0:T(1,128)S(1)}, /*...) while((s32[]{:T(128)}, ...), condition=%wide.region_7.8_spmd.clone, body=%wide.region_4.7_spmd.clone.sunk | while | flops 1100741120 | bytes 35732304 | solution.py:179
  255.5 69.2 %reduce-scatter.12.cloned.1.call-done = f32[256,2048]{1,0:T(8,128)} async-done(((f32[1024,2048]{1,0:T(8,128)}), f32[256,2048]{1,0:T(8,128)}) %reduce-scatter.12.cloned.1.call-update) | async-done | bytes 2097168 | tf_op jit(solution)/shard_map/reduce_scatter | solution.py:185
  334.3 52.7 %collective-permute-done = bf16[256,2048]{1,0:T(8,128)(2,1)S(1)} collective-permute-done((bf16[256,2048]{1,0:T(8,128)(2,1)S(1)}, bf16[256,2048]{1,0:T(8,128)(2,1)S(1)}, u32[]{:S(2)}, u32[]{:S(2)}) %collective-permute-start) | collective-permute-done | bytes 1048608 | tf_op jit(solution)/shard_map/ppermute | solution.py:108
  392.4 61.6 %collective-permute-done.2 = bf16[256,2048]{1,0:T(8,128)(2,1)} collective-permute-done((bf16[256,2048]{1,0:T(8,128)(2,1)S(1)}, bf16[256,2048]{1,0:T(8,128)(2,1)}, u32[]{:S(2)}, u32[]{:S(2)}) %collective-permute-start.2) | collective-permute-done | bytes 1048608 | tf_op jit(solution)/shard_map/ppermute | solution.py:108
  478.0 45.0 %collective-permute-done.4 = bf16[256,2048]{1,0:T(8,128)(2,1)S(1)} collective-permute-done((bf16[256,2048]{1,0:T(8,128)(2,1)}, bf16[256,2048]{1,0:T(8,128)(2,1)S(1)}, u32[]{:S(2)}, u32[]{:S(2)}) %collective-permute-start.4) | collective-permute-done | bytes 1048608 | tf_op jit(solution)/shard_map/ppermute | solution.py:108
  535.6 29.6 %collective-permute-done.6 = bf16[256,2048]{1,0:T(8,128)(2,1)S(1)} collective-permute-done((bf16[256,2048]{1,0:T(8,128)(2,1)S(1)}, bf16[256,2048]{1,0:T(8,128)(2,1)S(1)}, u32[]{:S(2)}, u32[]{:S(2)}) %collective-permute-start.6) | collective-permute-done | bytes 1048608 | tf_op jit(solution)/shard_map/ppermute | solution.py:108
  566.3 34.2 %all-gather.22.cloned.1.call-done = bf16[1024,2048]{1,0:T(8,128)(2,1)} async-done(((bf16[256,2048]{1,0:T(8,128)(2,1)}), bf16[1024,2048]{1,0:T(8,128)(2,1)}) %all-gather.22.cloned.1.call-update) | async-done | bytes 4194320 | tf_op jit(solution)/shard_map/all_gather | solution.py:189
  631.9 95.2 %all-gather.26.cloned.1.call-done = bf16[2048,2048]{1,0:T(8,128)(2,1)} async-done(((bf16[256,2048]{1,0:T(8,128)(2,1)}), bf16[2048,2048]{1,0:T(8,128)(2,1)}) %all-gather.26.cloned.1.call-update) | async-done | bytes 8388624 | tf_op jit(solution)/shard_map/all_gather | solution.py:129
  741.7 69.7 %reduce-scatter.14.cloned.1.call-done = f32[256,2048]{1,0:T(8,128)} async-done(((f32[1024,2048]{1,0:T(8,128)}), f32[256,2048]{1,0:T(8,128)}) %reduce-scatter.14.cloned.1.call-update) | async-done | bytes 2097168 | tf_op jit(solution)/shard_map/reduce_scatter | solution.py:196
  817.1 34.0 %all-gather.28.cloned.1.call-done = bf16[1024,2048]{1,0:T(8,128)(2,1)} async-done(((bf16[256,2048]{1,0:T(8,128)(2,1)}), bf16[1024,2048]{1,0:T(8,128)(2,1)}) %all-gather.28.cloned.1.call-update) | async-done | bytes 4194320 | tf_op jit(solution)/shard_map/all_gather | solution.py:215
  886.1 91.5 %all-gather.30.cloned.1.call-done = bf16[2048,2048]{1,0:T(8,128)(2,1)} async-done(((bf16[256,2048]{1,0:T(8,128)(2,1)}), bf16[2048,2048]{1,0:T(8,128)(2,1)}) %all-gather.30.cloned.1.call-update) | async-done | bytes 8388624 | tf_op jit(solution)/shard_map/all_gather | solution.py:206
  993.5 69.5 %reduce-scatter.16.cloned.1.call-done = f32[256,2048]{1,0:T(8,128)} async-done(((f32[1024,2048]{1,0:T(8,128)}), f32[256,2048]{1,0:T(8,128)}) %reduce-scatter.16.cloned.1.call-update) | async-done | bytes 2097168 | tf_op jit(solution)/shard_map/reduce_scatter | solution.py:225
  1126.9 68.7 %while.43 = (s32[]{:T(128)}, f32[1024,4,128]{0,2,1:T(8,128)S(1)}, f32[1024,4,128]{0,2,1:T(8,128)}, f32[2,512,4,128]{3,1,2,0:T(8,128)}, s32[2]{0:T(128)S(1)}, /*i...) while((s32[]{:T(128)}, f32[1024,4,128]{0,2,1:T(8,128)S(1)}, ...), condition=%wide.region_17.18_spmd.clone, body=%wide.region_15.17_spmd.clone.sunk | while | flops 2720266752 | bytes 163650544 | solution.py:272
  1274.3 130.0 %reduce-scatter.28.cloned.1.call-done = bf16[256,2048]{1,0:T(8,128)(2,1)} async-done(((bf16[2048,2048]{1,0:T(8,128)(2,1)}), bf16[256,2048]{1,0:T(8,128)(2,1)}) %reduce-scatter.28.cloned.1.call-update) | async-done | bytes 1048592 | tf_op jit(solution)/shard_map/reduce_scatter | solution.py:324
  1407.1 147.3 %reduce-scatter.30.cloned.1.call-done = bf16[256,2048]{1,0:T(8,128)(2,1)} async-done(((bf16[2048,2048]{1,0:T(8,128)(2,1)}), bf16[256,2048]{1,0:T(8,128)(2,1)}) %reduce-scatter.30.cloned.1.call-update) | async-done | bytes 1048592 | tf_op jit(solution)/shard_map/reduce_scatter | solution.py:327
  1557.2 40.7 %psum.39 = f32[4,2048]{1,0:T(4,128)} all-reduce(f32[4,2048]{1,0:T(4,128)S(1)} %pad_maximum_fusion.2), channel_id=1, replica_groups=mesh['fsdp'=8,'tp'=4] {'fsdp','tp'}, use_global_device_ids=true, to_apply=%region_34.35 | all-reduce | flops 8192 | bytes 65536 | tf_op jit(solution)/shard_map/psum | solution.py:339
  1597.9 28.4 %reduce-scatter.22.cloned.1.call-done = bf16[256,512]{0,1:T(8,128)(2,1)} async-done(((bf16[2048,512]{0,1:T(8,128)(2,1)}), bf16[256,512]{0,1:T(8,128)(2,1)}) %reduce-scatter.22.cloned.1.call-update) | async-done | bytes 262160 | tf_op jit(solution)/shard_map/reduce_scatter | solution.py:315
  1628.2 69.7 %reduce-scatter.20.cloned.1.call-done = bf16[256,512]{0,1:T(8,128)(2,1)} async-done(((bf16[2048,512]{0,1:T(8,128)(2,1)}), bf16[256,512]{0,1:T(8,128)(2,1)}) %reduce-scatter.20.cloned.1.call-update) | async-done | bytes 262160 | tf_op jit(solution)/shard_map/reduce_scatter | solution.py:312
  1699.8 68.9 %reduce-scatter.26.cloned.1.call-done = bf16[256,512]{1,0:T(8,128)(2,1)} async-done(((bf16[2048,512]{1,0:T(8,128)(2,1)}), bf16[256,512]{1,0:T(8,128)(2,1)}) %reduce-scatter.26.cloned.1.call-update) | async-done | bytes 262160 | tf_op jit(solution)/shard_map/reduce_scatter | solution.py:321
  1770.5 69.7 %reduce-scatter.24.cloned.1.call-done = bf16[256,512]{0,1:T(8,128)(2,1)} async-done(((bf16[2048,512]{0,1:T(8,128)(2,1)}), bf16[256,512]{0,1:T(8,128)(2,1)}) %reduce-scatter.24.cloned.1.call-update) | async-done | bytes 262160 | tf_op jit(solution)/shard_map/reduce_scatter | solution.py:318
  1842.1 44.3 %reduce-scatter.18.cloned.1.call-done = bf16[256,2048]{1,0:T(8,128)(2,1)} async-done(((bf16[1024,2048]{1,0:T(8,128)(2,1)}), bf16[256,2048]{1,0:T(8,128)(2,1)}) %reduce-scatter.18.cloned.1.call-update) | async-done | bytes 1048592 | tf_op jit(solution)/shard_map/reduce_scatter | solution.py:304
  (358 shorter events, 491.5 us)
Async XLA Ops:
  7.9 88.6 %all-gather.12.cloned.1.call-start = ((), (), s32[]{:S(2)}) async-start(), calls=%async_computation.11 | async-start | bytes 5242880 | tf_op jit(solution)/shard_map/all_gather | solution.py:91
  8.7 139.1 %all-gather.16.cloned.1.call-start = ((), (), s32[]{:S(2)}) async-start(), calls=%async_computation.13 | async-start | bytes 2359296 | tf_op jit(solution)/shard_map/all_gather | solution.py:124
  9.4 188.0 %all-gather.18.cloned.1.call-start = ((), (), s32[]{:S(2)}) async-start(), calls=%async_computation.14 | async-start | bytes 2359296 | tf_op jit(solution)/shard_map/all_gather | solution.py:125
  10.0 237.1 %all-gather.20.cloned.1.call-start = ((), (), s32[]{:S(2)}) async-start(), calls=%async_computation.15 | async-start | bytes 2359296 | tf_op jit(solution)/shard_map/all_gather | solution.py:126
  10.6 314.2 %reduce-scatter.12.cloned.1.call-start = ((), (), s32[]{:S(2)}) async-start(), calls=%async_computation.16 | async-start | bytes 10485760 | tf_op jit(solution)/shard_map/reduce_scatter | solution.py:185
  254.7 311.6 %all-gather.24.cloned.1.call-start = ((), (), s32[]{:S(2)}) async-start(), calls=%async_computation.18 | async-start | bytes 9437184 | tf_op jit(solution)/shard_map/all_gather | solution.py:127
  255.5 345.0 %all-gather.22.cloned.1.call-start = ((), (), s32[]{:S(2)}) async-start(), calls=%async_computation.17 | async-start | bytes 5242880 | tf_op jit(solution)/shard_map/all_gather | solution.py:189
  328.4 398.7 %all-gather.26.cloned.1.call-start = ((), (), s32[]{:S(2)}) async-start(), calls=%async_computation.19 | async-start | bytes 9437184 | tf_op jit(solution)/shard_map/all_gather | solution.py:129
  329.1 482.2 %reduce-scatter.14.cloned.1.call-start = ((), (), s32[]{:S(2)}) async-start(), calls=%async_computation.20 | async-start | bytes 10485760 | tf_op jit(solution)/shard_map/reduce_scatter | solution.py:196
  389.5 72.4 %collective-permute-start.3 = (bf16[256,2048]{1,0:T(8,128)(2,1)S(1)}, bf16[256,2048]{1,0:T(8,128)(2,1)}, u32[]{:S(2)}, u32[]{:S(2)}) collective-permute-start(bf16[256,2048]{1,0:T(8,128)(2,1)S(1)} %collective-permute-done.1), channel_id=1, source_target_pairs={{0,28},{4,0},{8,4},{12,8},{16,12},{20,16},{24,20},{28,24},{1,29},{... | collective-permute-start | bytes 3145736 | tf_op jit(solution)/shard_map/ppermute | solution.py:116
  453.9 69.0 %collective-permute-start.4 = (bf16[256,2048]{1,0:T(8,128)(2,1)}, bf16[256,2048]{1,0:T(8,128)(2,1)S(1)}, u32[]{:S(2)}, u32[]{:S(2)}) collective-permute-start(bf16[256,2048]{1,0:T(8,128)(2,1)} %collective-permute-done.2), channel_id=1, source_target_pairs={{0,4},{4,8},{8,12},{12,16},{16,20},{20,24},{24,28},{28,0},{1,5},{5... | collective-permute-start | bytes 3145736 | tf_op jit(solution)/shard_map/ppermute | solution.py:108
  461.9 72.6 %collective-permute-start.5 = (bf16[256,2048]{1,0:T(8,128)(2,1)}, bf16[256,2048]{1,0:T(8,128)(2,1)S(1)}, u32[]{:S(2)}, u32[]{:S(2)}) collective-permute-start(bf16[256,2048]{1,0:T(8,128)(2,1)} %collective-permute-done.3), channel_id=1, source_target_pairs={{0,28},{4,0},{8,4},{12,8},{16,12},{20,16},{24,20},{28,24},{1,29},{... | collective-permute-start | bytes 3145736 | tf_op jit(solution)/shard_map/ppermute | solution.py:116
  741.6 109.4 %all-gather.28.cloned.1.call-start = ((), (), s32[]{:S(2)}) async-start(), calls=%async_computation.21 | async-start | bytes 5242880 | tf_op jit(solution)/shard_map/all_gather | solution.py:215
  816.4 161.1 %all-gather.30.cloned.1.call-start = ((), (), s32[]{:S(2)}) async-start(), calls=%async_computation.22 | async-start | bytes 9437184 | tf_op jit(solution)/shard_map/all_gather | solution.py:206
  817.0 246.0 %reduce-scatter.16.cloned.1.call-start = ((), (), s32[]{:S(2)}) async-start(), calls=%async_computation.23 | async-start | bytes 10485760 | tf_op jit(solution)/shard_map/reduce_scatter | solution.py:225
  993.3 127.2 %all-gather.32.cloned.1.call-start = ((), (), s32[]{:S(2)}) async-start(), calls=%async_computation.24 | async-start | bytes 5242880 | tf_op jit(solution)/shard_map/all_gather | solution.py:230
  1068.6 202.9 %reduce-scatter.32.cloned.1.call-start = ((), (), s32[]{:S(2)}) async-start(), calls=%async_computation.32 | async-start | bytes 9437184 | tf_op jit(solution)/shard_map/reduce_scatter | solution.py:330
  1082.8 321.5 %reduce-scatter.28.cloned.1.call-start = ((), (), s32[]{:S(2)}) async-start(), calls=%async_computation.30 | async-start | bytes 9437184 | tf_op jit(solution)/shard_map/reduce_scatter | solution.py:324
  1096.9 457.4 %reduce-scatter.30.cloned.1.call-start = ((), (), s32[]{:S(2)}) async-start(), calls=%async_computation.31 | async-start | bytes 9437184 | tf_op jit(solution)/shard_map/reduce_scatter | solution.py:327
  1111.5 514.8 %reduce-scatter.22.cloned.1.call-start = ((), (), s32[]{:S(2)}) async-start(), calls=%async_computation.27 | async-start | bytes 2359296 | tf_op jit(solution)/shard_map/reduce_scatter | solution.py:315
  1237.4 460.5 %reduce-scatter.20.cloned.1.call-start = ((), (), s32[]{:S(2)}) async-start(), calls=%async_computation.26 | async-start | bytes 2359296 | tf_op jit(solution)/shard_map/reduce_scatter | solution.py:312
  1244.3 524.3 %reduce-scatter.26.cloned.1.call-start = ((), (), s32[]{:S(2)}) async-start(), calls=%async_computation.29 | async-start | bytes 2359296 | tf_op jit(solution)/shard_map/reduce_scatter | solution.py:321
  1250.9 589.3 %reduce-scatter.24.cloned.1.call-start = ((), (), s32[]{:S(2)}) async-start(), calls=%async_computation.28 | async-start | bytes 2359296 | tf_op jit(solution)/shard_map/reduce_scatter | solution.py:318
  1258.7 627.7 %reduce-scatter.18.cloned.1.call-start = ((), (), s32[]{:S(2)}) async-start(), calls=%async_computation.25 | async-start | bytes 5242880 | tf_op jit(solution)/shard_map/reduce_scatter | solution.py:304
  (82 other events, 2681.2 us)
Sparse Core Ops, SparseCore 0:
  10.1 51.7 all-gather.13
  63.5 32.9 all-gather.11
  98.7 49.0 all-gather.15
  149.8 47.6 all-gather.17
  199.4 47.6 all-gather.19
  254.8 69.9 reduce-scatter.11
  326.9 237.5 all-gather.23
  566.7 33.7 all-gather.21
  602.6 124.4 all-gather.25
  741.7 69.5 reduce-scatter.13
  816.6 34.4 all-gather.27
  853.0 124.4 all-gather.29
  993.4 69.5 reduce-scatter.15
  1068.7 34.4 all-gather.31
  1106.7 147.4 reduce-scatter.31
  1257.7 146.5 reduce-scatter.27
  1407.7 146.5 reduce-scatter.29
  1557.7 68.5 reduce-scatter.21
  1629.9 67.9 reduce-scatter.19
  1701.3 67.3 reduce-scatter.25
  1772.2 67.9 reduce-scatter.23
  1842.7 43.6 reduce-scatter.17
